TPU v7x, 32 devices: a whole 2x2x4 slice. The times are simulated.
32 devices in a mesh: chan: 4 (over z), pulse: 4 (over x, core), range: 2 (over y).
Axes of the slice: x: 2, y: 2, z: 4, core: 2. Of those that a mesh axis runs over, the one named last changes fastest.
Arguments:
- signal: bfloat16 [2, 64, 32, 8192], P(None, 'chan', 'pulse', 'range'), may hold values from -6 to 6
- steering: bfloat16 [2, 32, 64], replicated, may hold values from -0.5 to 0.5
- spectrum: float32 [2, 8192], replicated, may hold values from -6 to 6
Outputs:
- detection: float32 [32, 32, 8192], P('chan', 'pulse', 'range')
All inputs are finite; a program needn't handle non-finite values.
Results may differ from a plain program's by a relative error of at most 0.0087.
Values may be sent and summed in bfloat16 or wider, within the bound.
A program may use at most 64 MiB of HBM per device.

v0:
```python
import math
import jax
import jax.numpy as jnp
from jax import lax
from jax.sharding import PartitionSpec as P

GUARD = 4
TRAIN = 16
PRECISE = lax.Precision.HIGHEST
NOISE_FLOOR = 0.25


def padded_2(x, sides, width):
    for axis, dim in sides:
        peers, length = (lax.axis_size(axis), x.shape[dim])
        up = [(i, (i + 1) % peers) for i in range(peers - 1)]
        down = [(j, i) for i, j in up]
        last = lax.slice_in_dim(x, length - width, length, axis=dim)
        initial = lax.slice_in_dim(x, 0, width, axis=dim)
        before = lax.ppermute(last, axis, up)
        after = lax.ppermute(initial, axis, down)
        x = jnp.concatenate([before, x, after], axis=dim)
    return x


def doppler_tables(pulse_count):
    row_ids = lax.broadcasted_iota(jnp.int32, (pulse_count, pulse_count), 0)
    col_ids = lax.broadcasted_iota(jnp.int32, (pulse_count, pulse_count), 1)
    phase_angle = (row_ids * col_ids % pulse_count).astype(jnp.float32) * (
        2.0 * math.pi / pulse_count
    )
    norm_scale = 1.0 / math.sqrt(pulse_count)
    table_real = (jnp.cos(phase_angle) * norm_scale).astype(jnp.bfloat16)
    table_imag = (-jnp.sin(phase_angle) * norm_scale).astype(jnp.bfloat16)
    return (table_real, table_imag)


def phase_table(row_count, col_count, period_len, direction):
    row_ids = lax.broadcasted_iota(jnp.int32, (row_count, col_count), 0)
    col_ids = lax.broadcasted_iota(jnp.int32, (row_count, col_count), 1)
    phase_angle = (row_ids * col_ids % period_len).astype(jnp.float32) * (
        2.0 * math.pi / period_len
    )
    return (jnp.cos(phase_angle), direction * jnp.sin(phase_angle))


def rotate_by(field_pair, table_pair):
    return (
        field_pair[0] * table_pair[0] - field_pair[1] * table_pair[1],
        field_pair[0] * table_pair[1] + field_pair[1] * table_pair[0],
    )


def mix_blocks(table_pair, field_pair):

    def contract(table_part, field_part):
        return jnp.einsum("km,bpmn->bpkn", table_part, field_part, precision=PRECISE)

    return (
        contract(table_pair[0], field_pair[0]) - contract(table_pair[1], field_pair[1]),
        contract(table_pair[0], field_pair[1]) + contract(table_pair[1], field_pair[0]),
    )


def mix_lanes(field_pair, table_pair):

    def contract(field_part, table_part):
        return jnp.einsum("bpkm,mn->bpkn", field_part, table_part, precision=PRECISE)

    return (
        contract(field_pair[0], table_pair[0]) - contract(field_pair[1], table_pair[1]),
        contract(field_pair[0], table_pair[1]) + contract(field_pair[1], table_pair[0]),
    )


def local_transform(field_pair, direction):
    size_all = field_pair[0].shape[-1]
    blocks = size_all // 128
    leading = field_pair[0].shape[:-1]
    shaped = tuple((member.reshape(leading + (blocks, 128)) for member in field_pair))
    outer_table = phase_table(blocks, blocks, blocks, direction)
    twiddle = phase_table(blocks, 128, size_all, direction)
    inner_table = phase_table(128, 128, 128, direction)
    if direction < 0:
        shaped = mix_blocks(outer_table, shaped)
        shaped = rotate_by(shaped, twiddle)
        shaped = mix_lanes(shaped, inner_table)
    else:
        shaped = mix_lanes(shaped, inner_table)
        shaped = rotate_by(shaped, twiddle)
        shaped = mix_blocks(outer_table, shaped)
    return tuple((member.reshape(leading + (size_all,)) for member in shaped))


def stack_weights(w_real, w_imag):
    return jnp.concatenate(
        [jnp.concatenate([w_real, -w_imag], 1), jnp.concatenate([w_imag, w_real], 1)], 0
    )


def shards(signal, steering, spectrum):
    beam_count = steering.shape[1]
    chan_count = steering.shape[2]
    pulse_local = signal.shape[2]
    gate_count = signal.shape[3]
    stacked = stack_weights(steering[0], steering[1])
    samples = lax.all_to_all(signal, "chan", split_axis=2, concat_axis=1, tiled=True)
    pulses_here = samples.shape[2]
    gates_here = samples.shape[3]
    flat_samples = samples.reshape(2 * chan_count, pulses_here * gates_here)
    formed = jnp.dot(stacked, flat_samples, preferred_element_type=jnp.float32)
    formed = formed.astype(jnp.bfloat16).reshape(2, beam_count, pulses_here, gates_here)
    beam_data = lax.all_to_all(formed, "chan", split_axis=1, concat_axis=2, tiled=True)
    beam_local = beam_data.shape[1]
    range_count = lax.axis_size("range")
    range_index = lax.axis_index("range")
    full_length = gate_count * range_count
    inverse_scale = 1.0 / full_length
    shard_piece = lax.all_gather(beam_data, "range", axis=3, tiled=True)
    shard_count = shard_piece.shape[3] // gate_count
    members = shard_piece.astype(jnp.float32).reshape(
        2, beam_local, pulse_local, shard_count, gate_count
    )
    source = jnp.arange(shard_count, dtype=jnp.int32)
    phase_angle = (source * range_index % range_count).astype(jnp.float32) * (
        2.0 * math.pi / range_count
    )
    cos_part = jnp.cos(phase_angle)[:, None]
    sin_part = -jnp.sin(phase_angle)[:, None]
    sum_real = jnp.sum(members[0] * cos_part - members[1] * sin_part, axis=2)
    sum_imag = jnp.sum(members[0] * sin_part + members[1] * cos_part, axis=2)
    folded = (sum_real, sum_imag)
    gate_ids = lax.broadcasted_iota(jnp.int32, (gate_count,), 0)
    global_angle = (gate_ids * range_index % full_length).astype(jnp.float32) * (
        2.0 * math.pi / full_length
    )
    folded = rotate_by(folded, (jnp.cos(global_angle), -jnp.sin(global_angle)))
    spectrum_local = local_transform(folded, -1.0)
    response = spectrum.reshape(2, gate_count, range_count)
    response = lax.dynamic_index_in_dim(response, range_index, axis=2, keepdims=False)
    response = jnp.transpose(response.reshape(2, 128, gate_count // 128), (0, 2, 1)).reshape(
        2, gate_count
    )
    filtered = rotate_by(spectrum_local, (response[0], response[1]))
    restored = local_transform(filtered, 1.0)
    restored = rotate_by(restored, (jnp.cos(global_angle), jnp.sin(global_angle)))
    shard_piece = (
        lax.all_gather(restored[0], "range", axis=2, tiled=True),
        lax.all_gather(restored[1], "range", axis=2, tiled=True),
    )
    shard_count = shard_piece[0].shape[2] // gate_count
    rows_real = shard_piece[0].reshape(beam_local, pulse_local, shard_count, gate_count)
    rows_imag = shard_piece[1].reshape(beam_local, pulse_local, shard_count, gate_count)
    source = jnp.arange(shard_count, dtype=jnp.int32)
    phase_angle = (source * range_index % range_count).astype(jnp.float32) * (
        2.0 * math.pi / range_count
    )
    cos_part = jnp.cos(phase_angle)[:, None]
    sin_part = jnp.sin(phase_angle)[:, None]
    sum_real = jnp.sum(rows_real * cos_part - rows_imag * sin_part, axis=2)
    sum_imag = jnp.sum(rows_real * sin_part + rows_imag * cos_part, axis=2)
    compressed = jnp.stack([sum_real * inverse_scale, sum_imag * inverse_scale]).astype(
        jnp.bfloat16
    )
    pulse_total = pulse_local * lax.axis_size("pulse")
    dop_real, dop_imag = doppler_tables(pulse_total)
    columns = lax.all_to_all(compressed, "pulse", split_axis=3, concat_axis=2, tiled=True)

    def product(table_part, values):
        return jnp.einsum("fp,bpr->bfr", table_part, values, preferred_element_type=jnp.float32)

    mixed_real = product(dop_real, columns[0]) - product(dop_imag, columns[1])
    mixed_imag = product(dop_real, columns[1]) + product(dop_imag, columns[0])
    power_part = lax.all_to_all(
        mixed_real * mixed_real + mixed_imag * mixed_imag,
        "pulse",
        split_axis=1,
        concat_axis=2,
        tiled=True,
    )
    halo_width = GUARD + TRAIN
    padded = padded_2(power_part, (("range", 2),), halo_width)
    window_sum = jnp.zeros_like(power_part)
    for offset in range(1, TRAIN + 1):
        left_start = halo_width - GUARD - offset
        right_start = halo_width + GUARD + offset
        window_sum = (
            window_sum
            + padded[:, :, left_start : left_start + gate_count]
            + padded[:, :, right_start : right_start + gate_count]
        )
    noise_level = window_sum / (2.0 * TRAIN)
    return power_part / (noise_level + NOISE_FLOOR)


def solution(mesh):
    in_specs = (P(None, "chan", "pulse", "range"), P(), P())
    out_specs = P("chan", "pulse", "range")
    return jax.shard_map(shards, mesh=mesh, in_specs=in_specs, out_specs=out_specs, check_vma=False)
```

profile of v0, /device:TPU:0, one launch (start us, length us, event | category | flops | bytes accessed | tf_op | source)
XLA Modules:
  0.0 388.4 jit_solution(4963313028370823325)
XLA Ops:
  6.5 4.1 %copy.81 = bf16[2,16,8,4096]{3,1,0,2:T(8,128)(2,1)} copy(bf16[2,16,8,4096]{3,2,1,0:T(8,128)(2,1)} %param.3) | data formatting | bytes 4194304 | tf_op args[0]
  10.6 6.5 %all-to-all-start = ((bf16[2,16,8,4096]{3,1,0,2:T(8,128)(2,1)}), bf16[2,16,8,4096]{3,1,0,2:T(8,128)(2,1)S(1)}, u32[]{:S(2)}, u32[]{:S(2)}) async-start(bf16[2,16,8,4096]{3,1,0,2:T(8,128)(2,1)} %copy.81), calls=%async_computation | async-start | bytes 4194304 | tf_op jit(solution)/shard_map/all_to_all | solution.py:107
  17.1 48.2 %all-to-all-done = bf16[2,16,8,4096]{3,1,0,2:T(8,128)(2,1)S(1)} async-done(((bf16[2,16,8,4096]{3,1,0,2:T(8,128)(2,1)}), bf16[2,16,8,4096]{3,1,0,2:T(8,128)(2,1)S(1)}, u32[]{:S(2)}, u32[]{:S(2)}) %all-to-all-start) | async-done | bytes 2097184 | tf_op jit(solution)/shard_map/all_to_all | solution.py:107
  71.0 27.7 %all_to_all.66 = bf16[2,32,2,4096]{3,2,0,1:T(2,128)(2,1)S(1)} all-to-all(bf16[2,32,2,4096]{3,2,0,1:T(2,128)(2,1)S(1)} %copy.83), channel_id=1, replica_groups=mesh['chan'=4,'pulse'=4,'range'=2] {'chan'}, dimensions={1} | all-to-all | bytes 2097152 | tf_op jit(solution)/shard_map/all_to_all | solution.py:113
  100.6 6.4 %reshape.188 = f32[2,4096,2]{2,1,0:T(8,128)} reshape(f32[2,8192]{1,0:T(2,128)S(1)} %copy-done.1) | data formatting | bytes 131072 | tf_op jit(solution)/shard_map/reshape | solution.py:139
  107.0 4.7 %dynamic-slice_reduce_fusion = f32[2,4096]{1,0:T(2,128)S(1)} fusion(f32[2,4096,2]{2,1,0:T(8,128)} %reshape.188, s32[]{:T(128)S(6)} %select_n.134), kind=kLoop, calls=%fused_computation.31 | loop fusion | bytes 65540 | tf_op jit(solution)/shard_map/jit(dynamic_index_in_dim)/dynamic_slice | solution.py:140
  112.5 20.2 %all-gather.4.cloned.1.call-done = bf16[2,8,8,8192]{3,1,2,0:T(8,128)(2,1)} async-done(((bf16[2,8,8,4096]{3,1,2,0:T(8,128)(2,1)}), bf16[2,8,8,8192]{3,1,2,0:T(8,128)(2,1)}) %all-gather.4.cloned.1.call-update) | async-done | bytes 2097168 | tf_op jit(solution)/shard_map/all_gather | solution.py:119
  132.7 3.9 %fusion.271 = (f32[1,8,8,8192]{3,1,2,0:T(8,128)}, f32[1,8,8,8192]{3,1,2,0:T(8,128)}) fusion(bf16[2,8,8,8192]{3,1,2,0:T(8,128)(2,1)} %all-gather.4.cloned.1.call-done), kind=kLoop, calls=%fused_computation.365 | loop fusion | bytes 8388608 | tf_op jit(solution)/shard_map/slice | solution.py:130
  136.6 3.0 reshape.202
  139.7 4.4 %reshape.203 = f32[8,8,2,4096]{3,2,0,1:T(2,128)} reshape(f32[1,8,8,8192]{3,1,2,0:T(8,128)} %get-tuple-element.12) | data formatting | bytes 4194304 | tf_op jit(solution)/shard_map/squeeze | solution.py:130
  144.1 5.8 %subtract_reduce_fusion.1 = (f32[8,8,4096]{2,1,0:T(8,128)S(1)}, f32[8,8,4096]{2,1,0:T(8,128)S(1)}) fusion(f32[8,8,2,4096]{3,2,0,1:T(2,128)} %reshape.203, f32[8,8,2,4096]{3,2,0,1:T(2,128)S(1)} %reshape.202, f32[2]{0:T(128)S(1)} %get-tuple-element.24, f32[2]{0:T(128)S(1)} %get-tuple-element.23), kind=kLoop, calls=%fused_computation.35 | loop fusion | flops 3670016 | bytes 6291472 | tf_op jit(solution)/shard_map/reduce_sum | solution.py:130
  172.0 2.4 reshape.191
  180.4 32.5 %all-gather.6.cloned.1.call-done = f32[8,8,8192]{2,1,0:T(8,128)} async-done(((f32[8,8,4096]{2,1,0:T(8,128)}), f32[8,8,8192]{2,1,0:T(8,128)}) %all-gather.6.cloned.1.call-update) | async-done | bytes 2097168 | tf_op jit(solution)/shard_map/all_gather | solution.py:148
  212.9 34.7 %all-gather.8.cloned.1.call-done = f32[8,8,8192]{2,1,0:T(8,128)} async-done(((f32[8,8,4096]{2,1,0:T(8,128)}), f32[8,8,8192]{2,1,0:T(8,128)}) %all-gather.8.cloned.1.call-update) | async-done | bytes 2097168 | tf_op jit(solution)/shard_map/all_gather | solution.py:149
  247.6 3.2 subtract_reduce_fusion
  252.1 14.0 %copy.106 = bf16[2,8,8,4096]{2,1,0,3:T(8,128)(2,1)} copy(bf16[2,8,8,4096]{3,1,2,0:T(8,128)(2,1)S(1)} %pad_maximum_fusion.2) | data formatting | bytes 2097152 | tf_op jit(solution)/shard_map/stack | solution.py:162
  266.1 20.5 %reshape.205 = bf16[4,2,65536]{2,1,0:T(2,128)(2,1)S(1)} reshape(bf16[4096,2,8,8]{3,2,1,0:T(8,128)(2,1)} %bitcast.133) | data formatting | bytes 2097152
  286.6 17.2 %all_to_all.67 = bf16[4,2,65536]{2,1,0:T(2,128)(2,1)S(1)} all-to-all(bf16[4,2,65536]{2,1,0:T(2,128)(2,1)S(1)} %reshape.205), channel_id=1, replica_groups=mesh['chan'=4,'pulse'=4,'range'=2] {'pulse'}, dimensions={0} | all-to-all | bytes 2097152 | tf_op jit(solution)/shard_map/all_to_all | solution.py:167
  303.8 21.7 %reshape.206 = bf16[4096,2,8,8]{3,2,1,0:T(8,128)(2,1)} reshape(bf16[4,2,65536]{2,1,0:T(2,128)(2,1)S(1)} %all_to_all.67) | data formatting | bytes 2097152
  325.5 16.0 %copy.107 = bf16[2,8,8,4,1024]{4,2,3,1,0:T(8,128)(2,1)S(1)} copy(bf16[2,8,8,4,1024]{2,1,0,4,3:T(8,128)(2,1)} %bitcast.134) | data formatting | bytes 2097152 | tf_op jit(solution)/shard_map/all_to_all | solution.py:167
  343.6 16.9 %all_to_all.68 = f32[8,32,1024]{2,0,1:T(8,128)S(1)} all-to-all(f32[8,32,1024]{2,0,1:T(8,128)S(1)} %copy.108), channel_id=1, replica_groups=mesh['chan'=4,'pulse'=4,'range'=2] {'pulse'}, dimensions={1} | all-to-all | bytes 2097152 | tf_op jit(solution)/shard_map/all_to_all | solution.py:174
  361.2 2.4 collective-permute-start
  365.2 4.2 %collective-permute-done.1 = f32[8,8,20]{2,1,0:T(8,128)S(1)} collective-permute-done((f32[8,8,20]{2,1,0:T(8,128)S(1)}, f32[8,8,20]{2,1,0:T(8,128)S(1)}, u32[]{:S(2)}, u32[]{:S(2)}) %collective-permute-start.1) | collective-permute-done | bytes 5152 | tf_op jit(solution)/shard_map/ppermute | solution.py:21
  369.4 12.0 %fusion.14 = f32[8,8,4096]{2,1,0:T(8,128)} fusion(f32[8,8,4096]{2,1,0:T(8,128)S(1)} %bitcast.151, f32[8,8,20]{2,1,0:T(8,128)S(1)} %collective-permute-done.1, f32[8,8,20]{2,1,0:T(8,128)S(1)} %collective-permute-done), kind=kLoop, calls=%fused_computation.60 | loop fusion | flops 17301504 | bytes 2107392 | tf_op jit(solution)/shard_map/div | solution.py:193
  (63 shorter events, 42.0 us)
Async XLA Ops:
  10.6 6.5 %copy-start.2 = (bf16[2,32,64]{2,1,0:T(8,128)(2,1)S(1)}, bf16[2,32,64]{2,1,0:T(8,128)(2,1)}, u32[]{:S(2)}) copy-start(bf16[2,32,64]{2,1,0:T(8,128)(2,1)} %param.4) | copy-start | bytes 24580
  10.6 54.7 %all-to-all-start = ((bf16[2,16,8,4096]{3,1,0,2:T(8,128)(2,1)}), bf16[2,16,8,4096]{3,1,0,2:T(8,128)(2,1)S(1)}, u32[]{:S(2)}, u32[]{:S(2)}) async-start(bf16[2,16,8,4096]{3,1,0,2:T(8,128)(2,1)} %copy.81), calls=%async_computation | async-start | bytes 4194304 | tf_op jit(solution)/shard_map/all_to_all | solution.py:107
  17.1 115.6 %all-gather.4.cloned.1.call-start = ((), (), s32[]{:S(2)}) async-start(), calls=%async_computation.4 | async-start | bytes 3145728 | tf_op jit(solution)/shard_map/all_gather | solution.py:119
  99.3 1.3 copy-start.1
  100.4 112.5 %all-gather.6.cloned.1.call-start = ((), (), s32[]{:S(2)}) async-start(), calls=%async_computation.5 | async-start | bytes 3145728 | tf_op jit(solution)/shard_map/all_gather | solution.py:148
  176.5 1.5 copy-start
  179.7 67.9 %all-gather.8.cloned.1.call-start = ((), (), s32[]{:S(2)}) async-start(), calls=%async_computation.6 | async-start | bytes 3145728 | tf_op jit(solution)/shard_map/all_gather | solution.py:149
  361.2 4.0 %collective-permute-start = (f32[8,8,20]{2,1,0:T(8,128)S(1)}, f32[8,8,20]{2,1,0:T(8,128)S(1)}, u32[]{:S(2)}, u32[]{:S(2)}) collective-permute-start(f32[8,8,20]{2,1,0:T(8,128)S(1)} %get-tuple-element.13), channel_id=1, source_target_pairs={{0,1},{2,3},{4,5},{6,7},{8,9},{10,11},{12,13},{14,15},{16,17},{18,... | collective-permute-start | bytes 15368 | tf_op jit(solution)/shard_map/ppermute | solution.py:20
  363.6 5.8 %collective-permute-start.1 = (f32[8,8,20]{2,1,0:T(8,128)S(1)}, f32[8,8,20]{2,1,0:T(8,128)S(1)}, u32[]{:S(2)}, u32[]{:S(2)}) collective-permute-start(f32[8,8,20]{2,1,0:T(8,128)S(1)} %get-tuple-element.14), channel_id=1, source_target_pairs={{1,0},{3,2},{5,4},{7,6},{9,8},{11,10},{13,12},{15,14},{17,16},{19,... | collective-permute-start | bytes 15368 | tf_op jit(solution)/shard_map/ppermute | solution.py:21
Sparse Core Ops, SparseCore 0:
  100.5 32.1 all-gather.3
  179.8 33.0 all-gather.5
  214.5 33.0 all-gather.7
where the time goes:
time: 395 us; the launch traced here: 388 us
  waiting for transfers between devices  141 us (36%)
  local copies, waits for them, and re-layouts  112 us (28%)
  blocking collectives  61.8 us (16%)
  matrix products  24.9 us (6%)
  other arithmetic  24.3 us (6%)
  between operations  13.9 us (4%)
  starting transfers between devices  10.5 us (3%)
    unnamed x12, local copies, waits for them, and re-layouts  48.9 us
    all_to_all x1, waiting for transfers between devices, shards(): lax.all_to_all(signal, 'chan', split_axis=2, concat_axis=1, tiled=True)  48.2 us
    all_gather x1, waiting for transfers between devices, shards(): lax.all_gather(restored[1], 'range', axis=2, tiled=True)  34.7 us
    all_gather x1, waiting for transfers between devices, shards(): lax.all_gather(restored[0], 'range', axis=2, tiled=True)  32.5 us
    all_to_all x1, blocking collectives, shards(): lax.all_to_all(formed, 'chan', split_axis=1, concat_axis=2, tiled=True)  27.7 us
    all_gather x1, waiting for transfers between devices, shards(): shard_piece = lax.all_gather(beam_data, 'range', axis=3, tiled=True)  20.2 us
    all_to_all x1, blocking collectives, shards(): lax.all_to_all(compressed, 'pulse', split_axis=3, concat_axis=2, tiled=True)  17.2 us
    all_to_all x1, blocking collectives, shards(): lax.all_to_all(mixed_real * mixed_real + mixed_imag * mixed_imag, 'pulse'...  16.9 us
  transfers between devices with their start and end apart: 6, of which 6 were waited for; matrix products, arithmetic and copies ran while one was open for 3% of the time, Pallas kernels for 0%

commit v1 on v0

--- a/solution.py
+++ b/solution.py
@@ -8,6 +8,26 @@
 TRAIN = 16
 PRECISE = lax.Precision.HIGHEST
 NOISE_FLOOR = 0.25
+
+
+def sheet_recast(load, dim_i):
+    axis_tag = "range"
+    block_next, parts_out, piece_out = (
+        lax.axis_size(axis_tag),
+        lax.axis_index(axis_tag),
+        load.shape[dim_i],
+    )
+    carry_in, view_out = (load, 1)
+    while view_out < block_next:
+        by_rank = []
+        h = 0
+        while h < block_next:
+            by_rank.append((h, (h - view_out) % block_next))
+            h = h + 1
+        carry_in = jnp.concatenate([carry_in, lax.ppermute(carry_in, axis_tag, by_rank)], dim_i)
+        view_out = 2 * view_out
+    v1 = jnp.roll(carry_in, parts_out * piece_out, dim_i)
+    return v1
 
 
 def padded_2(x, sides, width):
@@ -145,7 +165,7 @@
     restored = local_transform(filtered, 1.0)
     restored = rotate_by(restored, (jnp.cos(global_angle), jnp.sin(global_angle)))
     shard_piece = (
-        lax.all_gather(restored[0], "range", axis=2, tiled=True),
+        sheet_recast(restored[0], 2),
         lax.all_gather(restored[1], "range", axis=2, tiled=True),
     )
     shard_count = shard_piece[0].shape[2] // gate_count

time: 395 us -> 371 us (0.939)
  waiting for transfers between devices: 141 us -> 118 us
    ppermute x0 -> x1, waiting for transfers between devices: none -> 40 us  [sheet_recast(): lax.ppermute(carry_in, axis_tag, by_rank)]
    all_gather x1 -> x0, waiting for transfers between devices: 32.5 us -> none  [shards(): lax.all_gather(restored[0], 'range', axis=2, tiled=True)]
    all_gather x1, waiting for transfers between devices: 34.7 us -> 5.36 us  [shards(): lax.all_gather(restored[1], 'range', axis=2, tiled=True)]
    unnamed x12 -> x10, local copies, waits for them, and re-layouts: 48.9 us -> 47.7 us
  transfers between devices with their start and end apart: 6 -> 6, of which waited for: 6 -> 6; matrix products, arithmetic and copies ran while one was open for 3% -> 4% of each run, Pallas kernels for 0% -> 0%
where the time goes in v1:
time: 371 us; the launch traced here: 364 us
  waiting for transfers between devices  118 us (32%)
  local copies, waits for them, and re-layouts  111 us (30%)
  blocking collectives  61.8 us (17%)
  matrix products  24.5 us (7%)
  other arithmetic  24 us (6%)
  between operations  14.2 us (4%)
  starting transfers between devices  10.9 us (3%)
    all_to_all x1, waiting for transfers between devices, shards(): lax.all_to_all(signal, 'chan', split_axis=2, concat_axis=1, tiled=True)  48.2 us
    unnamed x10, local copies, waits for them, and re-layouts  47.7 us
    ppermute x1, waiting for transfers between devices, sheet_recast(): lax.ppermute(carry_in, axis_tag, by_rank)  40 us
    all_to_all x1, blocking collectives, shards(): lax.all_to_all(formed, 'chan', split_axis=1, concat_axis=2, tiled=True)  27.7 us
    all_gather x1, waiting for transfers between devices, shards(): shard_piece = lax.all_gather(beam_data, 'range', axis=3, tiled=True)  20.2 us
    all_to_all x1, blocking collectives, shards(): lax.all_to_all(compressed, 'pulse', split_axis=3, concat_axis=2, tiled=True)  17.2 us
    all_to_all x1, blocking collectives, shards(): lax.all_to_all(mixed_real * mixed_real + mixed_imag * mixed_imag, 'pulse'...  16.9 us
    all_to_all x1, local copies, waits for them, and re-layouts, shards(): lax.all_to_all(compressed, 'pulse', split_axis=3, concat_axis=2, tiled=True)  16 us
  transfers between devices with their start and end apart: 6, of which 6 were waited for; matrix products, arithmetic and copies ran while one was open for 4% of the time, Pallas kernels for 0%

profile of v1, /device:TPU:0, one launch (start us, length us, event | category | flops | bytes accessed | tf_op | source)
XLA Modules:
  0.0 364.5 jit_solution(10016934210120024921)
XLA Ops:
  6.5 4.1 %copy.63 = bf16[2,16,8,4096]{3,1,0,2:T(8,128)(2,1)} copy(bf16[2,16,8,4096]{3,2,1,0:T(8,128)(2,1)} %param.3) | data formatting | bytes 4194304 | tf_op args[0]
  10.6 6.5 %all-to-all-start = ((bf16[2,16,8,4096]{3,1,0,2:T(8,128)(2,1)}), bf16[2,16,8,4096]{3,1,0,2:T(8,128)(2,1)S(1)}, u32[]{:S(2)}, u32[]{:S(2)}) async-start(bf16[2,16,8,4096]{3,1,0,2:T(8,128)(2,1)} %copy.63), calls=%async_computation | async-start | bytes 4194304 | tf_op jit(solution)/shard_map/all_to_all | solution.py:127
  17.1 48.2 %all-to-all-done = bf16[2,16,8,4096]{3,1,0,2:T(8,128)(2,1)S(1)} async-done(((bf16[2,16,8,4096]{3,1,0,2:T(8,128)(2,1)}), bf16[2,16,8,4096]{3,1,0,2:T(8,128)(2,1)S(1)}, u32[]{:S(2)}, u32[]{:S(2)}) %all-to-all-start) | async-done | bytes 2097184 | tf_op jit(solution)/shard_map/all_to_all | solution.py:127
  71.0 27.7 %all_to_all.66 = bf16[2,32,2,4096]{3,2,0,1:T(2,128)(2,1)S(1)} all-to-all(bf16[2,32,2,4096]{3,2,0,1:T(2,128)(2,1)S(1)} %copy.65), channel_id=1, replica_groups=mesh['chan'=4,'pulse'=4,'range'=2] {'chan'}, dimensions={1} | all-to-all | bytes 2097152 | tf_op jit(solution)/shard_map/all_to_all | solution.py:133
  100.6 6.4 %reshape.188 = f32[2,4096,2]{2,1,0:T(8,128)} reshape(f32[2,8192]{1,0:T(2,128)S(1)} %copy-done.1) | data formatting | bytes 131072 | tf_op jit(solution)/shard_map/reshape | solution.py:159
  107.0 4.7 %dynamic-slice_reduce_fusion = f32[2,4096]{1,0:T(2,128)S(1)} fusion(f32[2,4096,2]{2,1,0:T(8,128)} %reshape.188, s32[]{:T(128)S(6)} %select_n.146), kind=kLoop, calls=%fused_computation.35 | loop fusion | bytes 65540 | tf_op jit(solution)/shard_map/jit(dynamic_index_in_dim)/dynamic_slice | solution.py:160
  112.5 20.2 %all-gather.3.cloned.1.call-done = bf16[2,8,8,8192]{3,1,2,0:T(8,128)(2,1)} async-done(((bf16[2,8,8,4096]{3,1,2,0:T(8,128)(2,1)}), bf16[2,8,8,8192]{3,1,2,0:T(8,128)(2,1)}) %all-gather.3.cloned.1.call-update) | async-done | bytes 2097168 | tf_op jit(solution)/shard_map/all_gather | solution.py:139
  132.7 3.9 %fusion.278 = (f32[1,8,8,8192]{3,1,2,0:T(8,128)}, f32[1,8,8,8192]{3,1,2,0:T(8,128)}) fusion(bf16[2,8,8,8192]{3,1,2,0:T(8,128)(2,1)} %all-gather.3.cloned.1.call-done), kind=kLoop, calls=%fused_computation.372 | loop fusion | bytes 8388608 | tf_op jit(solution)/shard_map/slice | solution.py:150
  136.7 3.0 reshape.202
  139.7 4.4 %reshape.203 = f32[8,8,2,4096]{3,2,0,1:T(2,128)} reshape(f32[1,8,8,8192]{3,1,2,0:T(8,128)} %get-tuple-element.12) | data formatting | bytes 4194304 | tf_op jit(solution)/shard_map/squeeze | solution.py:150
  144.1 5.8 %subtract_reduce_fusion.1 = (f32[8,8,4096]{2,1,0:T(8,128)S(1)}, f32[8,8,4096]{2,1,0:T(8,128)S(1)}) fusion(f32[8,8,2,4096]{3,2,0,1:T(2,128)} %reshape.203, f32[8,8,2,4096]{3,2,0,1:T(2,128)S(1)} %reshape.202, f32[2]{0:T(128)S(1)} %get-tuple-element.20, f32[2]{0:T(128)S(1)} %get-tuple-element.19), kind=kLoop, calls=%fused_computation.42 | loop fusion | flops 3670016 | bytes 6291472 | tf_op jit(solution)/shard_map/reduce_sum | solution.py:150
  170.2 2.4 reshape.191
  178.2 40.0 %collective-permute-done = f32[8,8,4096]{2,1,0:T(8,128)} collective-permute-done((f32[8,8,4096]{2,1,0:T(8,128)S(1)}, f32[8,8,4096]{2,1,0:T(8,128)}, u32[]{:S(2)}, u32[]{:S(2)}) %collective-permute-start) | collective-permute-done | bytes 1048608 | tf_op jit(solution)/shard_map/ppermute | solution.py:27
  219.9 5.4 %all-gather.5.cloned.1.call-done = f32[8,8,8192]{2,1,0:T(8,128)} async-done(((f32[8,8,4096]{2,1,0:T(8,128)}), f32[8,8,8192]{2,1,0:T(8,128)}) %all-gather.5.cloned.1.call-update) | async-done | bytes 2097168 | tf_op jit(solution)/shard_map/all_gather | solution.py:169
  225.3 2.5 subtract_reduce_fusion
  228.0 13.8 %copy.80 = bf16[2,8,8,4096]{2,1,0,3:T(8,128)(2,1)} copy(bf16[2,8,8,4096]{3,2,1,0:T(8,128)(2,1)S(1)} %pad_maximum_fusion.2) | data formatting | bytes 2097152 | tf_op jit(solution)/shard_map/stack | solution.py:182
  241.8 20.5 %reshape.205 = bf16[4,2,65536]{2,1,0:T(2,128)(2,1)S(1)} reshape(bf16[4096,2,8,8]{3,2,1,0:T(8,128)(2,1)} %bitcast.154) | data formatting | bytes 2097152
  262.3 17.2 %all_to_all.67 = bf16[4,2,65536]{2,1,0:T(2,128)(2,1)S(1)} all-to-all(bf16[4,2,65536]{2,1,0:T(2,128)(2,1)S(1)} %reshape.205), channel_id=1, replica_groups=mesh['chan'=4,'pulse'=4,'range'=2] {'pulse'}, dimensions={0} | all-to-all | bytes 2097152 | tf_op jit(solution)/shard_map/all_to_all | solution.py:187
  279.5 21.7 %reshape.206 = bf16[4096,2,8,8]{3,2,1,0:T(8,128)(2,1)} reshape(bf16[4,2,65536]{2,1,0:T(2,128)(2,1)S(1)} %all_to_all.67) | data formatting | bytes 2097152
  301.3 16.0 %copy.81 = bf16[2,8,8,4,1024]{4,2,3,1,0:T(8,128)(2,1)S(1)} copy(bf16[2,8,8,4,1024]{2,1,0,4,3:T(8,128)(2,1)} %bitcast.155) | data formatting | bytes 2097152 | tf_op jit(solution)/shard_map/all_to_all | solution.py:187
  319.3 16.9 %all_to_all.68 = f32[8,32,1024]{2,0,1:T(8,128)S(1)} all-to-all(f32[8,32,1024]{2,0,1:T(8,128)S(1)} %copy.82), channel_id=1, replica_groups=mesh['chan'=4,'pulse'=4,'range'=2] {'pulse'}, dimensions={1} | all-to-all | bytes 2097152 | tf_op jit(solution)/shard_map/all_to_all | solution.py:194
  336.9 2.5 collective-permute-start.1
  340.9 4.2 %collective-permute-done.2 = f32[8,8,20]{2,1,0:T(8,128)S(1)} collective-permute-done((f32[8,8,20]{2,1,0:T(8,128)S(1)}, f32[8,8,20]{2,1,0:T(8,128)S(1)}, u32[]{:S(2)}, u32[]{:S(2)}) %collective-permute-start.2) | collective-permute-done | bytes 5152 | tf_op jit(solution)/shard_map/ppermute | solution.py:41
  345.2 12.0 %fusion.17 = f32[8,8,4096]{2,1,0:T(8,128)} fusion(f32[8,8,4096]{2,1,0:T(8,128)S(1)} %bitcast.173, f32[8,8,20]{2,1,0:T(8,128)S(1)} %collective-permute-done.2, f32[8,8,20]{2,1,0:T(8,128)S(1)} %collective-permute-done.1), kind=kLoop, calls=%fused_computation.67 | loop fusion | flops 17301504 | bytes 2107392 | tf_op jit(solution)/shard_map/div | solution.py:213
  (61 shorter events, 40.4 us)
Async XLA Ops:
  10.6 6.5 %copy-start.2 = (bf16[2,32,64]{2,1,0:T(8,128)(2,1)S(1)}, bf16[2,32,64]{2,1,0:T(8,128)(2,1)}, u32[]{:S(2)}) copy-start(bf16[2,32,64]{2,1,0:T(8,128)(2,1)} %param.4) | copy-start | bytes 24580
  10.6 54.7 %all-to-all-start = ((bf16[2,16,8,4096]{3,1,0,2:T(8,128)(2,1)}), bf16[2,16,8,4096]{3,1,0,2:T(8,128)(2,1)S(1)}, u32[]{:S(2)}, u32[]{:S(2)}) async-start(bf16[2,16,8,4096]{3,1,0,2:T(8,128)(2,1)} %copy.63), calls=%async_computation | async-start | bytes 4194304 | tf_op jit(solution)/shard_map/all_to_all | solution.py:127
  17.1 115.6 %all-gather.3.cloned.1.call-start = ((), (), s32[]{:S(2)}) async-start(), calls=%async_computation.4 | async-start | bytes 3145728 | tf_op jit(solution)/shard_map/all_gather | solution.py:139
  99.3 1.3 copy-start.1
  100.4 124.9 %all-gather.5.cloned.1.call-start = ((), (), s32[]{:S(2)}) async-start(), calls=%async_computation.5 | async-start | bytes 3145728 | tf_op jit(solution)/shard_map/all_gather | solution.py:169
  174.9 1.5 copy-start
  177.8 40.4 %collective-permute-start = (f32[8,8,4096]{2,1,0:T(8,128)S(1)}, f32[8,8,4096]{2,1,0:T(8,128)}, u32[]{:S(2)}, u32[]{:S(2)}) collective-permute-start(f32[8,8,4096]{2,1,0:T(8,128)S(1)} %get-tuple-element.9), channel_id=1, source_target_pairs={{0,1},{1,0},{2,3},{3,2},{4,5},{5,4},{6,7},{7,6},{8,9},{9,8},{10,11... | collective-permute-start | bytes 3145736 | tf_op jit(solution)/shard_map/ppermute | solution.py:27
  336.9 4.0 %collective-permute-start.1 = (f32[8,8,20]{2,1,0:T(8,128)S(1)}, f32[8,8,20]{2,1,0:T(8,128)S(1)}, u32[]{:S(2)}, u32[]{:S(2)}) collective-permute-start(f32[8,8,20]{2,1,0:T(8,128)S(1)} %get-tuple-element.13), channel_id=1, source_target_pairs={{0,1},{2,3},{4,5},{6,7},{8,9},{10,11},{12,13},{14,15},{16,17},{18,... | collective-permute-start | bytes 15368 | tf_op jit(solution)/shard_map/ppermute | solution.py:40
  339.4 5.8 %collective-permute-start.2 = (f32[8,8,20]{2,1,0:T(8,128)S(1)}, f32[8,8,20]{2,1,0:T(8,128)S(1)}, u32[]{:S(2)}, u32[]{:S(2)}) collective-permute-start(f32[8,8,20]{2,1,0:T(8,128)S(1)} %get-tuple-element.14), channel_id=1, source_target_pairs={{1,0},{3,2},{5,4},{7,6},{9,8},{11,10},{13,12},{15,14},{17,16},{19,... | collective-permute-start | bytes 15368 | tf_op jit(solution)/shard_map/ppermute | solution.py:41
Sparse Core Ops, SparseCore 0:
  100.5 32.1 all-gather.2
  177.9 47.3 all-gather.4
